TPU v7x, 32 devices: a whole 2x2x4 slice. The times are simulated.
32 devices in a mesh: tm: 8 (over z, x), lev: 4 (over y, core).
Axes of the slice: x: 2, y: 2, z: 4, core: 2. Of those that a mesh axis runs over, the one named last changes fastest.
Arguments:
- increment: float32 [8, 3, 8, 256, 512], P('tm', None, 'lev'), may hold values from -6 to 6
- multiplier: float32 [8, 3, 8, 256, 512], P('tm', None, 'lev'), may hold values from -6 to 6
- error_var: float32 [8, 3, 8, 256, 512], P('tm', None, 'lev'), may hold values from 0.1 to 1
- obs_cell: int32 [8, 8, 512], P('tm', 'lev'), may hold values from 0 to 131071
- obs_dual: float32 [8, 8, 512], P('tm', 'lev'), may hold values from -6 to 6
- obs_var: float32 [8, 8, 512], P('tm', 'lev'), may hold values from 0.5 to 2
- level_gain: float32 [8], P('lev'), may hold values from 0.5 to 1.5
- mean_depth: float32 [8], P('lev'), may hold values from 0.5 to 2
- chain_decay: float32 [8, 3, 8], P('tm', None, 'lev'), may hold values from 0 to 1
Outputs:
- dual_product: float32 [8, 3, 8, 256, 512], P('tm', None, 'lev')
- obs_product: float32 [8, 8, 512], P('tm', 'lev')
- state_block_product: float32 [8, 3, 8, 256, 512], P('tm', None, 'lev')
- chain_solution: float32 [8, 3, 8, 256, 512], P('tm', None, 'lev')
All inputs are finite; a program needn't handle non-finite values.
Results may differ from a plain program's by a relative error of at most 0.0001.
Values sent between devices are 32-bit elements; how exact they have to be, the bound alone decides.
A program may use at most 320 MiB of HBM per device.

v0:
```python
import functools
from typing import Any, NamedTuple

import jax
import jax.numpy as jnp
from jax import lax
from jax.experimental import pallas as pl
from jax.experimental.pallas import tpu as pltpu
from jax.sharding import PartitionSpec as P

TIME_STEP = 0.25
ROTATION_PARAM = 0.5
COUPLING = 0.25
HALF = TIME_STEP * ROTATION_PARAM
SPLIT = 2
PAD = 8
MESH_ID = pl.DeviceIdType.MESH


class Scratch(NamedTuple):
    inc: Any
    mult: Any
    work: Any
    b1: Any
    own: Any
    swap: Any
    tangent: Any
    adjoint: Any
    tangent_in: Any
    adjoint_in: Any
    carried: Any
    sent: Any
    relay_t: Any
    relay_a: Any
    sums: Any
    met: Any
    total: Any
    columns: Any
    added: Any
    decay: Any
    decay_in: Any
    own_send: Any
    own_recv: Any
    tan_send: Any
    tan_recv: Any
    adj_send: Any
    adj_recv: Any
    rt_send: Any
    rt_recv: Any
    ra_send: Any
    ra_recv: Any
    ch_send: Any
    ch_recv: Any
    dual_sem: Any
    block_sem: Any
    chain_sem: Any
    decay_send: Any
    decay_recv: Any
    loads: Any
    lev_send: Any
    lev_recv: Any


def pieces(rows):
    return SPLIT if rows % (8 * SPLIT) == 0 else 1


def block_rows(rows):
    part = rows // pieces(rows)
    return next(b for b in (32, 16, 8, part) if part % b == 0)


def up_y(a):
    lane = lax.broadcasted_iota(jnp.int32, a.shape, 1)
    return jnp.where(lane == a.shape[1] - 1, 0.0, pltpu.roll(a, a.shape[1] - 1, 1))


def down_y(a):
    lane = lax.broadcasted_iota(jnp.int32, a.shape, 1)
    return jnp.where(lane == 0, 0.0, pltpu.roll(a, 1, 1))


def up_x(a):
    return pltpu.roll(a, a.shape[0] - 1, 0)


def down_x(a):
    return pltpu.roll(a, 1, 0)


def kernel(
    n, size, increment, multiplier, error_var, obs_cell, obs_dual, obs_var, level_gain, mean_depth,
    chain_decay, dual_out, obs_out, block_out, chain_out, *scratch,
):
    b = Scratch(*scratch)
    fields, levels, rows, cols = increment.shape[1:]
    planes = fields * levels
    per = pieces(rows)
    chunks = planes * per
    part = rows // per
    step = block_rows(rows)
    wide = step + 2 * PAD

    s = lax.axis_index("tm")
    lev = lax.axis_index("lev")
    odd = s % 2
    even = odd == 0
    pair = s // 2
    pairs = n // 2
    partner = s + 1 - 2 * odd

    def adjoint_cut(k):
        return chunks * (pairs - 1 - k) // pairs

    def tangent_cut(k):
        return jnp.minimum(chunks, chunks * (k + 1) // pairs + 1)

    def loop(low, high, fn):
        lax.fori_loop(low, high, lambda c, z: (fn(c), z)[1], 0)

    def where_in(c):
        return c // per, pl.ds(pl.multiple_of((c % per) * part, 8), part)

    def piece(ref, c):
        p, r = where_in(c)
        return ref.at[p, r, :]

    def remote(src, dst, send, recv, where):
        return pltpu.make_async_remote_copy(
            src_ref=src, dst_ref=dst, send_sem=send, recv_sem=recv, device_id=where, device_id_type=MESH_ID,
        )

    def move(src, dst, send, recv, c, to):
        return remote(piece(src, c), piece(dst, c), send.at[c], recv.at[c], {"tm": to})

    def lev_move(src, dst, i, to):
        return remote(src, dst, b.lev_send.at[i], b.lev_recv.at[i], {"lev": to})

    def own_copy(c):
        return move(b.own, b.swap, b.own_send, b.own_recv, c, partner)

    def tangent_copy(c):
        return move(b.tangent, b.tangent_in, b.tan_send, b.tan_recv, c, s + 1)

    def adjoint_copy(c):
        return move(b.adjoint, b.adjoint_in, b.adj_send, b.adj_recv, c, s - 1)

    def chain_copy(c):
        return move(b.sent, b.carried, b.ch_send, b.ch_recv, c, s + 2)

    def tangent_leg(c, to):
        return move(b.tangent, b.relay_t, b.tan_send, b.rt_recv, c, to)

    def tangent_turn(c, to):
        return move(b.relay_t, b.tangent_in, b.rt_send, b.tan_recv, c, to)

    def adjoint_leg(c, to):
        return move(b.adjoint, b.relay_a, b.adj_send, b.ra_recv, c, to)

    def adjoint_turn(c, to):
        return move(b.relay_a, b.adjoint_in, b.ra_send, b.adj_recv, c, to)

    def result_copy(src, out, sems, c):
        p, r = where_in(c)
        return pltpu.make_async_copy(piece(src, c), out.at[0, p // levels, p % levels, r, :], sems.at[c])

    def dual_copy(c):
        return result_copy(b.tangent_in, dual_out, b.dual_sem, c)

    def chain_result(c):
        return result_copy(b.carried, chain_out, b.chain_sem, c)

    def block_copy(c):
        return result_copy(b.adjoint_in, block_out, b.block_sem, c)

    decay_copy = remote(b.decay, b.decay_in, b.decay_send.at[0], b.decay_recv.at[0], {"tm": s - 1})

    def load(i, p):
        src = (increment, multiplier, error_var)[i]
        dst = (b.inc, b.mult, b.work)[i]
        return pltpu.make_async_copy(
            src.at[0, p // levels, p % levels], dst.at[p, pl.ds(PAD, rows), :], b.loads.at[i * planes + p]
        )

    for p in range(planes):
        for i in range(3):
            load(i, p).start()

    barrier = pltpu.get_barrier_semaphore()
    near = ((s >= 1, s - 1), (s >= 2, s - 2), (s < n - 1, s + 1), (s < n - 2, s + 2))
    for there, who in near:
        @pl.when(there)
        def _():
            pl.semaphore_signal(barrier, inc=1, device_id={"tm": who}, device_id_type=MESH_ID)
    bits = []
    bit = 1
    while bit < size:
        bits.append(bit)
        bit *= 2

    def across(bit):
        return lev + bit - 2 * bit * ((lev // bit) % 2)

    for bit in bits:
        pl.semaphore_signal(barrier, inc=1, device_id={"lev": across(bit)}, device_id_type=MESH_ID)

    def edges(ref, planes):
        zero = jnp.zeros((PAD, cols), jnp.float32)
        for p in range(planes):
            ref[p, pl.ds(0, PAD), :] = zero
            ref[p, pl.ds(PAD + rows, PAD), :] = zero

    for ref in (b.inc, b.mult, b.work, b.b1):
        edges(ref, planes)
    edges(b.columns, 4)
    for f in range(fields):
        for l in range(levels):
            b.decay[f * levels + l] = jnp.full((1, 128), chain_decay[0, f, l], jnp.float32)

    def own_at(c):
        p, r = where_in(c)

        @pl.when(c % per == 0)
        def _():
            for i in range(3):
                load(i, p).wait()

        inner = pl.ds(pl.multiple_of((c % per) * part + PAD, 8), part)
        b.own[p, r, :] = b.work[p, inner, :] * b.mult[p, inner, :] + b.inc[p, inner, :]

    gives_own = jnp.logical_or(even, s < n - 1)

    def give_own(c):
        @pl.when(gives_own)
        def _():
            own_copy(c).start()

    own_at(0)
    pl.semaphore_wait(barrier, len(bits) + sum(there.astype(jnp.int32) for there, _ in near))

    def own_next(c):
        own_at(c)
        give_own(c - 1)

    loop(1, chunks, own_next)
    give_own(chunks - 1)

    @pl.when(s >= 1)
    def _():
        decay_copy.start()

    def row_index(r0):
        return lax.broadcasted_iota(jnp.int32, (wide, cols), 0) + (r0 - PAD)

    def forward(h, u, v, column, r0, gain, depth):
        p = gain * h
        if column is not None:
            p = p + COUPLING * column
        u_new = u + TIME_STEP * (ROTATION_PARAM * v - (up_x(p) - p))
        v_new = v - TIME_STEP * (ROTATION_PARAM * u + (up_y(p) - p))
        u_new = jnp.where(row_index(r0) < 0, 0.0, u_new)
        h_new = h - TIME_STEP * depth * ((u_new - down_x(u_new)) + (v_new - down_y(v_new)))
        return h_new, u_new, v_new

    def back(h, u, v, r0, gain, depth):
        w = depth * h
        u2 = u + TIME_STEP * (up_x(w) - w)
        v2 = v + TIME_STEP * (up_y(w) - w)
        u2 = jnp.where(row_index(r0) < 0, 0.0, u2)
        p = TIME_STEP * ((u2 - down_x(u2)) + (v2 - down_y(v2)))
        return h + gain * p, u2 - HALF * v2, v2 + HALF * u2, p

    def middle(a):
        return a[PAD:PAD + step]

    def state_at(ref, l, r0):
        at = pl.ds(r0, wide)
        return ref[l, at, :], ref[levels + l, at, :], ref[2 * levels + l, at, :]

    def sweep(fn):
        loop(0, rows // step, lambda i: fn(pl.multiple_of(i * step, 8)))

    def put(ref, l, r0, values):
        for f, value in enumerate(values):
            ref[f * levels + l, pl.ds(r0, step), :] = middle(value)

    def put_padded(ref, l, r0, values):
        put(ref, l, r0 + PAD, values)

    sums = b.sums

    def ahead(r0):
        c0 = c1 = None
        for l in range(levels):
            h, u, v = state_at(b.inc, l, r0)
            h_new, _, _ = forward(h, u, v, None, r0, level_gain[l], mean_depth[l])
            c0 = middle(h) if c0 is None else c0 + middle(h)
            c1 = middle(h_new) if c1 is None else c1 + middle(h_new)
        sums[0, pl.ds(r0, step), :] = c0
        sums[0, pl.ds(rows + r0, step), :] = c1

    def behind(source, to):
        def fn(r0):
            bar = None
            for l in range(levels):
                h, u, v = state_at(source, l, r0)
                h2, u2, v2, p = back(h, u, v, r0, level_gain[l], mean_depth[l])
                if to == 0:
                    put_padded(b.b1, l, r0, (h2, u2, v2))
                bar = middle(p) if bar is None else bar + middle(p)
            sums[1, pl.ds(to * rows + r0, step), :] = COUPLING * bar
        return fn

    sweep(ahead)
    sweep(behind(b.mult, 0))
    sweep(behind(b.b1, 1))
    depth_sum = mean_depth[0]
    for l in range(1, levels):
        depth_sum = depth_sum + mean_depth[l]
    for k in range(2):
        sums[k, pl.ds(2 * rows, PAD), :] = jnp.full((PAD, cols), depth_sum, jnp.float32)

    half = lev % 2
    tall = 2 * rows + PAD
    total = b.total

    def meet_copy():
        return lev_move(sums.at[1 - half], b.met.at[0], 0, across(1))

    def add_met(slot, first):
        def fn(r0):
            at = pl.ds(r0, PAD)
            kept = sums[half, at, :] if first else total[at, :]
            total[at, :] = kept + b.met[slot, at, :]
        loop(0, tall // PAD, lambda i: fn(pl.multiple_of(i * PAD, 8)))

    meet = meet_copy()
    meet.start()
    meet.wait()
    add_met(0, True)

    def observe():
        count = obs_cell.shape[2]
        if cols & (cols - 1) == 0:
            shift = cols.bit_length() - 1

            def split(cells):
                return cells >> shift, cells & (cols - 1)
        else:
            def split(cells):
                return lax.div(cells, cols), lax.rem(cells, cols)

        row = lax.broadcasted_iota(jnp.int32, (rows, count), 0)
        col = lax.broadcasted_iota(jnp.int32, (cols, count), 0)
        for l in range(levels):
            at_row, at_col = split(obs_cell[0, pl.ds(l, 1), :])
            values = obs_dual[0, pl.ds(l, 1), :]
            hit_row = jnp.where(row == at_row, 1.0, 0.0)
            hit_col = jnp.where(col == at_col, 1.0, 0.0)
            seen = lax.dot_general(
                b.inc[l, pl.ds(PAD, rows), :], hit_col, (((1,), (0,)), ((), ())),
                precision=lax.Precision.HIGHEST, preferred_element_type=jnp.float32,
            )
            picked = jnp.sum(hit_row * seen, axis=0, keepdims=True)
            obs_out[0, pl.ds(l, 1), :] = obs_var[0, pl.ds(l, 1), :] * values + picked
            b.added[l] = lax.dot_general(
                hit_row * values, hit_col, (((1,), (1,)), ((), ())),
                precision=lax.Precision.HIGHEST, preferred_element_type=jnp.float32,
            )

    for i, bit in enumerate(bits[1:], 1):
        far = lev_move(total, b.met.at[i], i, across(bit))
        far.start()
        if i == 1:
            observe()
        far.wait()
        add_met(i, False)
    if len(bits) < 2:
        observe()

    columns = b.columns

    def first_column(r0):
        columns[2 * half, pl.ds(r0 + PAD, step), :] = total[pl.ds(r0, step), :]

    def second_column(r0):
        c = columns[2 * half, pl.ds(r0, wide), :]
        gx = jnp.where(row_index(r0) < 0, 0.0, up_x(c) - c)
        gy = up_y(c) - c
        lap = (gx - down_x(gx)) + (gy - down_y(gy))
        scale = (TIME_STEP * TIME_STEP * COUPLING) * total[pl.ds(2 * rows, 1), pl.ds(0, 1)]
        columns[2 * half + 1, pl.ds(r0 + PAD, step), :] = total[pl.ds(rows + r0, step), :] + scale * middle(lap)

    sweep(first_column)
    sweep(second_column)
    mine = columns.at[pl.ds(2 * half, 2)]
    near_copy = lev_move(mine, mine, len(bits), across(1))
    near_copy.start()
    near_copy.wait()

    def last_back(r0):
        at = pl.ds(r0, wide)
        bar0, bar1 = columns[2, at, :], columns[3, at, :]
        for l in range(levels):
            h, u, v = state_at(b.b1, l, r0)
            h2, u2, v2, _ = back(h + bar0, u, v, r0, level_gain[l], mean_depth[l])
            put(b.adjoint, l, r0, (h2 + bar1, u2, v2))

    def first_forward(r0):
        column = columns[0, pl.ds(r0, wide), :]
        for l in range(levels):
            h, u, v = state_at(b.inc, l, r0)
            put_padded(b.work, l, r0, forward(h, u, v, column, r0, level_gain[l], mean_depth[l]))

    def last_forward(r0):
        column = columns[1, pl.ds(r0, wide), :]
        for l in range(levels):
            h, u, v = state_at(b.work, l, r0)
            put(b.tangent, l, r0, forward(h, u, v, column, r0, level_gain[l], mean_depth[l]))

    sweep(last_back)
    below = pair - 1
    down_cut = adjoint_cut(below)
    across_cut = adjoint_cut(pair)

    @pl.when(jnp.logical_and(even, s >= 2))
    def _():
        loop(0, down_cut, lambda c: adjoint_leg(c, s - 2).start())
        loop(down_cut, chunks, lambda c: adjoint_leg(c, s + 1).start())

    sweep(first_forward)
    sweep(last_forward)
    up_cut = tangent_cut(pair)
    here_cut = tangent_cut(below)
    climbs = jnp.logical_and(odd == 1, s < n - 1)

    @pl.when(even)
    def _():
        loop(0, chunks, lambda c: tangent_copy(c).start())

    @pl.when(climbs)
    def _():
        loop(0, up_cut, lambda c: tangent_leg(c, s + 2).start())
        loop(up_cut, chunks, lambda c: tangent_leg(c, s - 1).start())

    @pl.when(s < n - 1)
    def _():
        decay_copy.wait_recv()

    def chain_step(c):
        p, r = where_in(c)
        d = chain_decay[0, p // levels, p % levels]

        @pl.when(s >= 1)
        def _():
            tangent_copy(c).wait_recv()

        @pl.when(s == 0)
        def _():
            b.tangent_in[p, r, :] = jnp.zeros((part, cols), jnp.float32)

        @pl.when(s >= 2)
        def _():
            chain_copy(c).wait_recv()

        @pl.when(s < 2)
        def _():
            b.carried[p, r, :] = jnp.zeros((part, cols), jnp.float32)

        @pl.when(jnp.logical_or(odd == 1, s < n - 2))
        def _():
            own_copy(c).wait_recv()

        swap = b.swap[p, r, :]
        product = b.own[p, r, :] - b.tangent_in[p, r, :]
        here = d * (b.carried[p, r, :] + jnp.where(odd == 1, swap, 0.0)) + product
        b.tangent_in[p, r, :] = product
        b.carried[p, r, :] = here

        @pl.when(s < n - 2)
        def _():
            d_next = b.decay_in[p][:, :1]
            b.sent[p, r, :] = d_next * here + (jnp.where(even, swap, 0.0) - b.tangent[p, r, :])
            chain_copy(c).start()

        dual_copy(c).start()
        chain_result(c).start()

    loop(0, jnp.where(s == 0, chunks, 0), chain_step)

    @pl.when(jnp.logical_and(even, s < n - 2))
    def _():
        def turn_up(c):
            tangent_leg(c, s - 1).wait_recv()
            tangent_turn(c, s + 2).start()

        def turn_across(c):
            adjoint_leg(c, s - 2).wait_recv()
            adjoint_turn(c, s + 1).start()

        loop(up_cut, chunks, turn_up)
        loop(0, across_cut, turn_across)

    @pl.when(odd == 1)
    def _():
        @pl.when(s >= 3)
        def _():
            def turn_across(c):
                tangent_leg(c, s + 2).wait_recv()
                tangent_turn(c, s - 1).start()

            loop(0, here_cut, turn_across)

        loop(0, chunks, lambda c: adjoint_copy(c).start())

        @pl.when(s >= 3)
        def _():
            def turn_down(c):
                adjoint_leg(c, s + 1).wait_recv()
                adjoint_turn(c, s - 2).start()

            loop(down_cut, chunks, turn_down)

    loop(0, jnp.where(s == 0, 0, chunks), chain_step)

    def block_step(i):
        c = lax.rem(i + across_cut * odd, chunks)
        p, r = where_in(c)
        inner = pl.ds(pl.multiple_of((c % per) * part + PAD, 8), part)

        @pl.when(s < n - 1)
        def _():
            adjoint_copy(c).wait_recv()

        kept = b.mult[p, inner, :] - jnp.where(s < n - 1, b.adjoint_in[p, r, :], 0.0)
        b.adjoint_in[p, r, :] = kept

        @pl.when(p < levels)
        def _():
            b.adjoint_in[p, r, :] = kept + b.added[jnp.minimum(p, levels - 1), r, :]

        block_copy(c).start()

    loop(0, chunks, block_step)

    @pl.when(gives_own)
    def _():
        loop(0, chunks, lambda c: own_copy(c).wait_send())

    @pl.when(s < n - 1)
    def _():
        loop(0, chunks, lambda c: tangent_copy(c).wait_send())

    @pl.when(s >= 1)
    def _():
        loop(0, chunks, lambda c: adjoint_copy(c).wait_send())
        decay_copy.wait_send()

    @pl.when(jnp.logical_and(even, s < n - 2))
    def _():
        loop(up_cut, chunks, lambda c: tangent_turn(c, s + 2).wait_send())
        loop(0, across_cut, lambda c: adjoint_turn(c, s + 1).wait_send())

    @pl.when(jnp.logical_and(odd == 1, s >= 3))
    def _():
        loop(0, here_cut, lambda c: tangent_turn(c, s - 1).wait_send())
        loop(down_cut, chunks, lambda c: adjoint_turn(c, s - 2).wait_send())

    @pl.when(s < n - 2)
    def _():
        loop(0, chunks, lambda c: chain_copy(c).wait_send())

    loop(0, chunks, lambda c: dual_copy(c).wait())
    loop(0, chunks, lambda c: chain_result(c).wait())
    loop(0, chunks, lambda c: block_copy(c).wait())


def shards(
    increment, multiplier, error_var, obs_cell, obs_dual, obs_var,
    level_gain, mean_depth, chain_decay,
):
    n = lax.axis_size("tm")
    size = lax.axis_size("lev")
    if n % 2 or size < 2 or size & (size - 1):
        raise ValueError("unsupported mesh")
    _, fields, levels, rows, cols = increment.shape
    planes = fields * levels
    chunks = planes * pieces(rows)
    rounds = size.bit_length() - 1
    tall = 2 * rows + PAD

    def room(*shape):
        return pltpu.VMEM(shape, jnp.float32)

    def flags(count):
        return pltpu.SemaphoreType.DMA((count,))

    scratch = Scratch(
        *[room(planes, rows + 2 * PAD, cols)] * 4,
        *[room(planes, rows, cols)] * 10,
        room(2, tall, cols), room(rounds, tall, cols), room(tall, cols),
        room(4, rows + 2 * PAD, cols), room(levels, rows, cols),
        room(planes, 1, 128), room(planes, 1, 128),
        *[flags(chunks)] * 15,
        flags(1), flags(1), flags(3 * planes), flags(rounds + 1), flags(rounds + 1),
    )
    state = jax.ShapeDtypeStruct(increment.shape, jnp.float32)
    place = pl.BlockSpec(memory_space=pl.ANY)
    small = pl.BlockSpec(memory_space=pltpu.VMEM)
    scalar = pl.BlockSpec(memory_space=pltpu.SMEM)
    return pl.pallas_call(
        functools.partial(kernel, n, size),
        out_shape=[state, jax.ShapeDtypeStruct(obs_dual.shape, jnp.float32), state, state],
        in_specs=[place] * 3 + [small] * 3 + [scalar] * 3,
        out_specs=[place, small, place, place],
        scratch_shapes=list(scratch),
        compiler_params=pltpu.CompilerParams(
            collective_id=0, has_side_effects=True, vmem_limit_bytes=63 * 1024 * 1024
        ),
    )(
        increment, multiplier, error_var, obs_cell, obs_dual, obs_var,
        level_gain, mean_depth, chain_decay,
    )


def solution(mesh):
    state = P("tm", None, "lev", None, None)
    obs = P("tm", "lev", None)
    return jax.shard_map(
        shards,
        mesh=mesh,
        in_specs=(state, state, state, obs, obs, obs, P("lev"), P("lev"), P("tm", None, "lev")),
        out_specs=(state, obs, state, state),
        check_vma=False,
    )
```

profile of v0, /device:TPU:24, one launch (start us, length us, event | category | flops | bytes accessed | tf_op | source)
XLA Modules:
  0.0 214.9 jit_solution(7959527229211543122)
XLA Ops:
  0.6 1.3 copy.13.chain_decay
  2.0 203.3 %shard_map.120 = (f32[1,3,2,256,512]{4,3,2,1,0:T(8,128)}, f32[1,2,512]{2,1,0:T(2,128)}, f32[1,3,2,256,512]{4,3,2,1,0:T(8,128)}, f32[1,3,2,256,512]{4,3,2,1,0:T(8,128)}) custom-call(f32[1,3,2,256,512]{4,3,2,1,0:T(8,128)} %increment.1, f32[1,3,2,256,512]{4,3,2,1,0:T(8,128)} %multiplier.1, f32[1,3,2,256,512]{4,3,2,1,0:T(8,128)} %error_var.1, ...), custom_call_target="tpu_custom_call" | custom-call | tf_op jit(solution)/shard_map/pallas_call | solution.py:611
  205.3 0.0 copy-start.2
  205.3 0.0 copy-start.1
  205.3 4.3 %copy.18 = f32[1,3,2,256,512]{4,3,2,1,0:T(8,128)} copy(f32[1,3,2,256,512]{4,3,2,1,0:T(8,128)} %get-tuple-element.8) | data formatting | bytes 6291456
  209.6 0.0 copy-done.2
  209.6 0.6 copy.19
  210.2 0.0 copy-done.1
  210.2 0.0 copy-start
  210.2 1.7 copy.20
  211.8 1.4 copy-done
  213.2 1.7 copy.21
Async XLA Ops:
  205.3 4.3 %copy-start.2 = (f32[1,2,512]{2,1,0:T(2,128)S(1)}, f32[1,2,512]{2,1,0:T(2,128)}, u32[]{:S(2)}) copy-start(f32[1,2,512]{2,1,0:T(2,128)} %get-tuple-element.9) | copy-start | bytes 12292
  205.3 4.9 %copy-start.1 = (f32[1,3,2,256,512]{4,3,2,1,0:T(8,128)S(1)}, f32[1,3,2,256,512]{4,3,2,1,0:T(8,128)}, u32[]{:S(2)}) copy-start(f32[1,3,2,256,512]{4,3,2,1,0:T(8,128)} %get-tuple-element.10) | copy-start | bytes 9437188
  210.2 3.0 %copy-start = (f32[1,3,2,256,512]{4,3,2,1,0:T(8,128)S(1)}, f32[1,3,2,256,512]{4,3,2,1,0:T(8,128)}, u32[]{:S(2)}) copy-start(f32[1,3,2,256,512]{4,3,2,1,0:T(8,128)} %get-tuple-element.11) | copy-start | bytes 9437188
where the time goes:
time: 215 us
  Pallas kernels  203 us (94%)
  local copies, waits for them, and re-layouts  10.9 us (5%)
    pallas_call x1, Pallas kernels, shards(): pl.pallas_call(functools.partial(kernel, n, size), out_shape=[state, jax....  203 us
    unnamed x11, local copies, waits for them, and re-layouts  10.9 us

commit v1 on v0

--- a/solution.py
+++ b/solution.py
@@ -26,9 +26,6 @@
     swap: Any
     tangent: Any
     adjoint: Any
-    tangent_in: Any
-    adjoint_in: Any
-    carried: Any
     sent: Any
     relay_t: Any
     relay_a: Any
@@ -51,9 +48,6 @@
     ra_recv: Any
     ch_send: Any
     ch_recv: Any
-    dual_sem: Any
-    block_sem: Any
-    chain_sem: Any
     decay_send: Any
     decay_recv: Any
     loads: Any
@@ -90,7 +84,7 @@
 
 def kernel(
     n, size, increment, multiplier, error_var, obs_cell, obs_dual, obs_var, level_gain, mean_depth,
-    chain_decay, dual_out, obs_out, block_out, chain_out, *scratch,
+    chain_decay, tangent_in, obs_out, adjoint_in, carried, *scratch,
 ):
     b = Scratch(*scratch)
     fields, levels, rows, cols = increment.shape[1:]
@@ -140,38 +134,25 @@
         return move(b.own, b.swap, b.own_send, b.own_recv, c, partner)
 
     def tangent_copy(c):
-        return move(b.tangent, b.tangent_in, b.tan_send, b.tan_recv, c, s + 1)
+        return move(b.tangent, tangent_in, b.tan_send, b.tan_recv, c, s + 1)
 
     def adjoint_copy(c):
-        return move(b.adjoint, b.adjoint_in, b.adj_send, b.adj_recv, c, s - 1)
+        return move(b.adjoint, adjoint_in, b.adj_send, b.adj_recv, c, s - 1)
 
     def chain_copy(c):
-        return move(b.sent, b.carried, b.ch_send, b.ch_recv, c, s + 2)
+        return move(b.sent, carried, b.ch_send, b.ch_recv, c, s + 2)
 
     def tangent_leg(c, to):
         return move(b.tangent, b.relay_t, b.tan_send, b.rt_recv, c, to)
 
     def tangent_turn(c, to):
-        return move(b.relay_t, b.tangent_in, b.rt_send, b.tan_recv, c, to)
+        return move(b.relay_t, tangent_in, b.rt_send, b.tan_recv, c, to)
 
     def adjoint_leg(c, to):
         return move(b.adjoint, b.relay_a, b.adj_send, b.ra_recv, c, to)
 
     def adjoint_turn(c, to):
-        return move(b.relay_a, b.adjoint_in, b.ra_send, b.adj_recv, c, to)
-
-    def result_copy(src, out, sems, c):
-        p, r = where_in(c)
-        return pltpu.make_async_copy(piece(src, c), out.at[0, p // levels, p % levels, r, :], sems.at[c])
-
-    def dual_copy(c):
-        return result_copy(b.tangent_in, dual_out, b.dual_sem, c)
-
-    def chain_result(c):
-        return result_copy(b.carried, chain_out, b.chain_sem, c)
-
-    def block_copy(c):
-        return result_copy(b.adjoint_in, block_out, b.block_sem, c)
+        return move(b.relay_a, adjoint_in, b.ra_send, b.adj_recv, c, to)
 
     decay_copy = remote(b.decay, b.decay_in, b.decay_send.at[0], b.decay_recv.at[0], {"tm": s - 1})
 
@@ -215,7 +196,7 @@
     edges(b.columns, 4)
     for f in range(fields):
         for l in range(levels):
-            b.decay[f * levels + l] = jnp.full((1, 128), chain_decay[0, f, l], jnp.float32)
+            b.decay[f * levels + l] = jnp.full((1, 128), chain_decay[0, l, f], jnp.float32)
 
     def own_at(c):
         p, r = where_in(c)
@@ -235,19 +216,21 @@
         def _():
             own_copy(c).start()
 
-    own_at(0)
-    pl.semaphore_wait(barrier, len(bits) + sum(there.astype(jnp.int32) for there, _ in near))
+    with jax.named_scope("greet"):
+        own_at(0)
+        pl.semaphore_wait(barrier, len(bits) + sum(there.astype(jnp.int32) for there, _ in near))
+
+    @pl.when(s >= 1)
+    def _():
+        decay_copy.start()
 
     def own_next(c):
         own_at(c)
         give_own(c - 1)
 
-    loop(1, chunks, own_next)
-    give_own(chunks - 1)
-
-    @pl.when(s >= 1)
-    def _():
-        decay_copy.start()
+    with jax.named_scope("own"):
+        loop(1, chunks, own_next)
+        give_own(chunks - 1)
 
     def row_index(r0):
         return lax.broadcasted_iota(jnp.int32, (wide, cols), 0) + (r0 - PAD)
@@ -311,9 +294,11 @@
             sums[1, pl.ds(to * rows + r0, step), :] = COUPLING * bar
         return fn
 
-    sweep(ahead)
-    sweep(behind(b.mult, 0))
-    sweep(behind(b.b1, 1))
+    with jax.named_scope("ahead"):
+        sweep(ahead)
+    with jax.named_scope("behind"):
+        sweep(behind(b.mult, 0))
+        sweep(behind(b.b1, 1))
     depth_sum = mean_depth[0]
     for l in range(1, levels):
         depth_sum = depth_sum + mean_depth[l]
@@ -335,9 +320,10 @@
         loop(0, tall // PAD, lambda i: fn(pl.multiple_of(i * PAD, 8)))
 
     meet = meet_copy()
-    meet.start()
-    meet.wait()
-    add_met(0, True)
+    with jax.named_scope("meet"):
+        meet.start()
+        meet.wait()
+        add_met(0, True)
 
     def observe():
         count = obs_cell.shape[2]
@@ -372,9 +358,11 @@
         far = lev_move(total, b.met.at[i], i, across(bit))
         far.start()
         if i == 1:
-            observe()
-        far.wait()
-        add_met(i, False)
+            with jax.named_scope("observe"):
+                observe()
+        with jax.named_scope("far"):
+            far.wait()
+            add_met(i, False)
     if len(bits) < 2:
         observe()
 
@@ -391,12 +379,14 @@
         scale = (TIME_STEP * TIME_STEP * COUPLING) * total[pl.ds(2 * rows, 1), pl.ds(0, 1)]
         columns[2 * half + 1, pl.ds(r0 + PAD, step), :] = total[pl.ds(rows + r0, step), :] + scale * middle(lap)
 
-    sweep(first_column)
-    sweep(second_column)
+    with jax.named_scope("column"):
+        sweep(first_column)
+        sweep(second_column)
     mine = columns.at[pl.ds(2 * half, 2)]
     near_copy = lev_move(mine, mine, len(bits), across(1))
-    near_copy.start()
-    near_copy.wait()
+    with jax.named_scope("near"):
+        near_copy.start()
+        near_copy.wait()
 
     def last_back(r0):
         at = pl.ds(r0, wide)
@@ -418,7 +408,8 @@
             h, u, v = state_at(b.work, l, r0)
             put(b.tangent, l, r0, forward(h, u, v, column, r0, level_gain[l], mean_depth[l]))
 
-    sweep(last_back)
+    with jax.named_scope("back"):
+        sweep(last_back)
     below = pair - 1
     down_cut = adjoint_cut(below)
     across_cut = adjoint_cut(pair)
@@ -428,8 +419,9 @@
         loop(0, down_cut, lambda c: adjoint_leg(c, s - 2).start())
         loop(down_cut, chunks, lambda c: adjoint_leg(c, s + 1).start())
 
-    sweep(first_forward)
-    sweep(last_forward)
+    with jax.named_scope("forward"):
+        sweep(first_forward)
+        sweep(last_forward)
     up_cut = tangent_cut(pair)
     here_cut = tangent_cut(below)
     climbs = jnp.logical_and(odd == 1, s < n - 1)
@@ -449,7 +441,7 @@
 
     def chain_step(c):
         p, r = where_in(c)
-        d = chain_decay[0, p // levels, p % levels]
+        d = chain_decay[0, p % levels, p // levels]
 
         @pl.when(s >= 1)
         def _():
@@ -457,7 +449,7 @@
 
         @pl.when(s == 0)
         def _():
-            b.tangent_in[p, r, :] = jnp.zeros((part, cols), jnp.float32)
+            tangent_in[p, r, :] = jnp.zeros((part, cols), jnp.float32)
 
         @pl.when(s >= 2)
         def _():
@@ -465,17 +457,17 @@
 
         @pl.when(s < 2)
         def _():
-            b.carried[p, r, :] = jnp.zeros((part, cols), jnp.float32)
+            carried[p, r, :] = jnp.zeros((part, cols), jnp.float32)
 
         @pl.when(jnp.logical_or(odd == 1, s < n - 2))
         def _():
             own_copy(c).wait_recv()
 
         swap = b.swap[p, r, :]
-        product = b.own[p, r, :] - b.tangent_in[p, r, :]
-        here = d * (b.carried[p, r, :] + jnp.where(odd == 1, swap, 0.0)) + product
-        b.tangent_in[p, r, :] = product
-        b.carried[p, r, :] = here
+        product = b.own[p, r, :] - tangent_in[p, r, :]
+        here = d * (carried[p, r, :] + jnp.where(odd == 1, swap, 0.0)) + product
+        tangent_in[p, r, :] = product
+        carried[p, r, :] = here
 
         @pl.when(s < n - 2)
         def _():
@@ -483,10 +475,8 @@
             b.sent[p, r, :] = d_next * here + (jnp.where(even, swap, 0.0) - b.tangent[p, r, :])
             chain_copy(c).start()
 
-        dual_copy(c).start()
-        chain_result(c).start()
-
-    loop(0, jnp.where(s == 0, chunks, 0), chain_step)
+    with jax.named_scope("chain0"):
+        loop(0, jnp.where(s == 0, chunks, 0), chain_step)
 
     @pl.when(jnp.logical_and(even, s < n - 2))
     def _():
@@ -498,8 +488,10 @@
             adjoint_leg(c, s - 2).wait_recv()
             adjoint_turn(c, s + 1).start()
 
-        loop(up_cut, chunks, turn_up)
-        loop(0, across_cut, turn_across)
+        with jax.named_scope("turn_up"):
+            loop(up_cut, chunks, turn_up)
+        with jax.named_scope("turn_over"):
+            loop(0, across_cut, turn_across)
 
     @pl.when(odd == 1)
     def _():
@@ -509,7 +501,8 @@
                 tangent_leg(c, s + 2).wait_recv()
                 tangent_turn(c, s - 1).start()
 
-            loop(0, here_cut, turn_across)
+            with jax.named_scope("turn_back"):
+                loop(0, here_cut, turn_across)
 
         loop(0, chunks, lambda c: adjoint_copy(c).start())
 
@@ -519,9 +512,11 @@
                 adjoint_leg(c, s + 1).wait_recv()
                 adjoint_turn(c, s - 2).start()
 
-            loop(down_cut, chunks, turn_down)
-
-    loop(0, jnp.where(s == 0, 0, chunks), chain_step)
+            with jax.named_scope("turn_down"):
+                loop(down_cut, chunks, turn_down)
+
+    with jax.named_scope("chain"):
+        loop(0, jnp.where(s == 0, 0, chunks), chain_step)
 
     def block_step(i):
         c = lax.rem(i + across_cut * odd, chunks)
@@ -532,47 +527,55 @@
         def _():
             adjoint_copy(c).wait_recv()
 
-        kept = b.mult[p, inner, :] - jnp.where(s < n - 1, b.adjoint_in[p, r, :], 0.0)
-        b.adjoint_in[p, r, :] = kept
+        kept = b.mult[p, inner, :] - jnp.where(s < n - 1, adjoint_in[p, r, :], 0.0)
+        adjoint_in[p, r, :] = kept
 
         @pl.when(p < levels)
         def _():
-            b.adjoint_in[p, r, :] = kept + b.added[jnp.minimum(p, levels - 1), r, :]
-
-        block_copy(c).start()
-
-    loop(0, chunks, block_step)
-
-    @pl.when(gives_own)
-    def _():
-        loop(0, chunks, lambda c: own_copy(c).wait_send())
-
-    @pl.when(s < n - 1)
-    def _():
-        loop(0, chunks, lambda c: tangent_copy(c).wait_send())
-
-    @pl.when(s >= 1)
-    def _():
-        loop(0, chunks, lambda c: adjoint_copy(c).wait_send())
-        decay_copy.wait_send()
-
-    @pl.when(jnp.logical_and(even, s < n - 2))
-    def _():
-        loop(up_cut, chunks, lambda c: tangent_turn(c, s + 2).wait_send())
-        loop(0, across_cut, lambda c: adjoint_turn(c, s + 1).wait_send())
-
-    @pl.when(jnp.logical_and(odd == 1, s >= 3))
-    def _():
-        loop(0, here_cut, lambda c: tangent_turn(c, s - 1).wait_send())
-        loop(down_cut, chunks, lambda c: adjoint_turn(c, s - 2).wait_send())
-
-    @pl.when(s < n - 2)
-    def _():
-        loop(0, chunks, lambda c: chain_copy(c).wait_send())
-
-    loop(0, chunks, lambda c: dual_copy(c).wait())
-    loop(0, chunks, lambda c: chain_result(c).wait())
-    loop(0, chunks, lambda c: block_copy(c).wait())
+            adjoint_in[p, r, :] = kept + b.added[jnp.minimum(p, levels - 1), r, :]
+
+    with jax.named_scope("block"):
+        loop(0, chunks, block_step)
+
+    with jax.named_scope("drain"):
+        @pl.when(gives_own)
+        def _():
+            loop(0, chunks, lambda c: own_copy(c).wait_send())
+
+        @pl.when(s < n - 1)
+        def _():
+            loop(0, chunks, lambda c: tangent_copy(c).wait_send())
+
+        @pl.when(s >= 1)
+        def _():
+            loop(0, chunks, lambda c: adjoint_copy(c).wait_send())
+            decay_copy.wait_send()
+
+        @pl.when(jnp.logical_and(even, s < n - 2))
+        def _():
+            loop(up_cut, chunks, lambda c: tangent_turn(c, s + 2).wait_send())
+            loop(0, across_cut, lambda c: adjoint_turn(c, s + 1).wait_send())
+
+        @pl.when(jnp.logical_and(odd == 1, s >= 3))
+        def _():
+            loop(0, here_cut, lambda c: tangent_turn(c, s - 1).wait_send())
+            loop(down_cut, chunks, lambda c: adjoint_turn(c, s - 2).wait_send())
+
+        @pl.when(s < n - 2)
+        def _():
+            loop(0, chunks, lambda c: chain_copy(c).wait_send())
+
+
+def write_out(dual_in, seen_in, block_in, chain_in, dual, seen, block, chain, sems):
+    planes = dual.shape[0]
+    copies = [pltpu.make_async_copy(seen_in, seen, sems.at[3 * planes])]
+    for i, (src, dst) in enumerate(((dual_in, dual), (block_in, block), (chain_in, chain))):
+        for p in range(planes):
+            copies.append(pltpu.make_async_copy(src.at[p], dst.at[p], sems.at[i * planes + p]))
+    for copy in copies:
+        copy.start()
+    for copy in copies:
+        copy.wait()
 
 
 def shards(
@@ -597,29 +600,40 @@
 
     scratch = Scratch(
         *[room(planes, rows + 2 * PAD, cols)] * 4,
-        *[room(planes, rows, cols)] * 10,
+        *[room(planes, rows, cols)] * 7,
         room(2, tall, cols), room(rounds, tall, cols), room(tall, cols),
         room(4, rows + 2 * PAD, cols), room(levels, rows, cols),
         room(planes, 1, 128), room(planes, 1, 128),
-        *[flags(chunks)] * 15,
+        *[flags(chunks)] * 12,
         flags(1), flags(1), flags(3 * planes), flags(rounds + 1), flags(rounds + 1),
     )
-    state = jax.ShapeDtypeStruct(increment.shape, jnp.float32)
     place = pl.BlockSpec(memory_space=pl.ANY)
     small = pl.BlockSpec(memory_space=pltpu.VMEM)
     scalar = pl.BlockSpec(memory_space=pltpu.SMEM)
-    return pl.pallas_call(
+    held = pltpu.VMEM((planes, rows, cols), jnp.float32)
+    results = pl.pallas_call(
         functools.partial(kernel, n, size),
-        out_shape=[state, jax.ShapeDtypeStruct(obs_dual.shape, jnp.float32), state, state],
+        out_shape=[held, pltpu.VMEM(obs_dual.shape, jnp.float32), held, held],
         in_specs=[place] * 3 + [small] * 3 + [scalar] * 3,
-        out_specs=[place, small, place, place],
+        out_specs=[small] * 4,
         scratch_shapes=list(scratch),
         compiler_params=pltpu.CompilerParams(
-            collective_id=0, has_side_effects=True, vmem_limit_bytes=63 * 1024 * 1024
+            collective_id=0, has_side_effects=True, vmem_limit_bytes=50 * 1024 * 1024
         ),
     )(
         increment, multiplier, error_var, obs_cell, obs_dual, obs_var,
-        level_gain, mean_depth, chain_decay,
+        level_gain, mean_depth, jnp.swapaxes(chain_decay, 1, 2),
+    )
+    dual, seen, block, chain = pl.pallas_call(
+        write_out,
+        out_shape=[jax.ShapeDtypeStruct(r.shape, jnp.float32) for r in results],
+        in_specs=[small] * 4,
+        out_specs=[place] * 4,
+        scratch_shapes=[flags(3 * planes + 1)],
+        compiler_params=pltpu.CompilerParams(vmem_limit_bytes=1024 * 1024),
+    )(*[pltpu.with_memory_space_constraint(r, pltpu.VMEM) for r in results])
+    return (
+        dual.reshape(increment.shape), seen, block.reshape(increment.shape), chain.reshape(increment.shape),
     )
 
 

time: 215 us -> 196 us (0.912)
  local copies, waits for them, and re-layouts: 10.9 us -> 0 us
  Pallas kernels: 203 us -> 193 us
    unnamed x11 -> x0, local copies, waits for them, and re-layouts: 10.9 us -> none
    pallas_call x1 -> x2, Pallas kernels: 203 us -> 193 us  [the longest x1 189 us: shards(): pl.pallas_call(functools.partial(kernel, n, size), out_shape=[held, pltpu...]
where the time goes in v1:
time: 196 us; the launch traced here: 194 us
  Pallas kernels  193 us (98%)
    pallas_call x1, Pallas kernels, shards(): pl.pallas_call(functools.partial(kernel, n, size), out_shape=[held, pltpu...  189 us

profile of v1, /device:TPU:24, one launch (start us, length us, event | category | flops | bytes accessed | tf_op | source)
XLA Modules:
  0.0 193.9 jit_solution(11077983763677267543)
XLA Ops:
  0.6 189.5 %shard_map.120 = (f32[6,256,512]{2,1,0:T(8,128)S(1)}, f32[1,2,512]{2,1,0:T(2,128)S(1)}, f32[6,256,512]{2,1,0:T(8,128)S(1)}, f32[6,256,512]{2,1,0:T(8,128)S(1)}) custom-call(f32[1,3,2,256,512]{4,3,2,1,0:T(8,128)} %increment.1, f32[1,3,2,256,512]{4,3,2,1,0:T(8,128)} %multiplier.1, f32[1,3,2,256,512]{4,3,2,1,0:T(8,128)} %error_var.1, s32[1,2,512]{2,1,0:T(2,128)} %obs_cell.1, ...), custom_call_target="tpu_custom_call" | custom-call | tf_op jit(solution)/shard_map/pallas_call | solution.py:614
  190.1 3.8 %shard_map.121 = (f32[6,256,512]{2,1,0:T(8,128)}, f32[1,2,512]{2,1,0:T(2,128)}, f32[6,256,512]{2,1,0:T(8,128)}, f32[6,256,512]{2,1,0:T(8,128)}) custom-call(f32[6,256,512]{2,1,0:T(8,128)S(1)} %get-tuple-element.12.dual_in, f32[1,2,512]{2,1,0:T(2,128)S(1)} %get-tuple-element.13.seen_in, f32[6,256,512]{2,1,0:T(8,128)S(1)} %get-tuple-element.14.block_in, ...), custom_call_target="tpu_custom_call" | custom-call | tf_op jit(solution)/shard_map/pallas_call | solution.py:627

commit v2 on v1

--- a/solution.py
+++ b/solution.py
@@ -36,21 +36,26 @@
     added: Any
     decay: Any
     decay_in: Any
-    own_send: Any
+    decay_relay: Any
+    cells: Any
+    obs_dual: Any
+    obs_var: Any
+    gain: Any
+    depth: Any
+    chain_decay: Any
+    sends: Any
     own_recv: Any
-    tan_send: Any
+    loads: Any
     tan_recv: Any
-    adj_send: Any
     adj_recv: Any
     rt_send: Any
     rt_recv: Any
     ra_send: Any
     ra_recv: Any
-    ch_send: Any
     ch_recv: Any
     decay_send: Any
     decay_recv: Any
-    loads: Any
+    small_loads: Any
     lev_send: Any
     lev_recv: Any
 
@@ -83,10 +88,12 @@
 
 
 def kernel(
-    n, size, increment, multiplier, error_var, obs_cell, obs_dual, obs_var, level_gain, mean_depth,
-    chain_decay, tangent_in, obs_out, adjoint_in, carried, *scratch,
+    n, size, increment, multiplier, error_var, cell_at, obs_dual_at, obs_var_at, gain_at, depth_at,
+    decay_at, tangent_in, obs_out, adjoint_in, carried, *scratch,
 ):
     b = Scratch(*scratch)
+    obs_cell, obs_dual, obs_var = b.cells, b.obs_dual, b.obs_var
+    level_gain, mean_depth, chain_decay = b.gain, b.depth, b.chain_decay
     fields, levels, rows, cols = increment.shape[1:]
     planes = fields * levels
     per = pieces(rows)
@@ -107,7 +114,7 @@
         return chunks * (pairs - 1 - k) // pairs
 
     def tangent_cut(k):
-        return jnp.minimum(chunks, chunks * (k + 1) // pairs + 1)
+        return jnp.minimum(chunks, chunks * (k + 1) // max(pairs - 1, 1))
 
     def loop(low, high, fn):
         lax.fori_loop(low, high, lambda c, z: (fn(c), z)[1], 0)
@@ -125,50 +132,55 @@
         )
 
     def move(src, dst, send, recv, c, to):
-        return remote(piece(src, c), piece(dst, c), send.at[c], recv.at[c], {"tm": to})
+        return remote(piece(src, c), piece(dst, c), send, recv.at[c], {"tm": to})
 
     def lev_move(src, dst, i, to):
         return remote(src, dst, b.lev_send.at[i], b.lev_recv.at[i], {"lev": to})
 
     def own_copy(c):
-        return move(b.own, b.swap, b.own_send, b.own_recv, c, partner)
+        return remote(piece(b.own, c), piece(b.swap, c), b.sends.at[0], b.own_recv.at[c // per], {"tm": partner})
+
+    def own_plane(p):
+        return remote(b.own.at[p], b.swap.at[p], b.sends.at[0], b.own_recv.at[p], {"tm": partner})
+
+    def all_sent(src, dst, i):
+        remote(src, dst, b.sends.at[i], b.own_recv.at[0], {"tm": partner}).wait_send()
 
     def tangent_copy(c):
-        return move(b.tangent, tangent_in, b.tan_send, b.tan_recv, c, s + 1)
+        return move(b.tangent, tangent_in, b.sends.at[1], b.tan_recv, c, s + 1)
 
     def adjoint_copy(c):
-        return move(b.adjoint, adjoint_in, b.adj_send, b.adj_recv, c, s - 1)
+        return move(b.adjoint, adjoint_in, b.sends.at[2], b.adj_recv, c, s - 1)
 
     def chain_copy(c):
-        return move(b.sent, carried, b.ch_send, b.ch_recv, c, s + 2)
+        return move(b.sent, carried, b.sends.at[3], b.ch_recv, c, s + 2)
 
     def tangent_leg(c, to):
-        return move(b.tangent, b.relay_t, b.tan_send, b.rt_recv, c, to)
+        return move(b.tangent, b.relay_t, b.sends.at[1], b.rt_recv, c, to)
 
     def tangent_turn(c, to):
-        return move(b.relay_t, tangent_in, b.rt_send, b.tan_recv, c, to)
+        return move(b.relay_t, tangent_in, b.rt_send.at[c], b.tan_recv, c, to)
 
     def adjoint_leg(c, to):
-        return move(b.adjoint, b.relay_a, b.adj_send, b.ra_recv, c, to)
+        return move(b.adjoint, b.relay_a, b.sends.at[2], b.ra_recv, c, to)
 
     def adjoint_turn(c, to):
-        return move(b.relay_a, adjoint_in, b.ra_send, b.adj_recv, c, to)
+        return move(b.relay_a, adjoint_in, b.ra_send.at[c], b.adj_recv, c, to)
 
     decay_copy = remote(b.decay, b.decay_in, b.decay_send.at[0], b.decay_recv.at[0], {"tm": s - 1})
+    decay_leg = remote(b.decay, b.decay_relay, b.decay_send.at[0], b.decay_recv.at[1], {"tm": s - 2})
+    decay_turn = remote(b.decay_relay, b.decay_in, b.decay_send.at[1], b.decay_recv.at[0], {"tm": s + 1})
+    turns = jnp.logical_and(even, s < n - 2)
 
     def load(i, p):
         src = (increment, multiplier, error_var)[i]
         dst = (b.inc, b.mult, b.work)[i]
         return pltpu.make_async_copy(
-            src.at[0, p // levels, p % levels], dst.at[p, pl.ds(PAD, rows), :], b.loads.at[i * planes + p]
+            src.at[0, p // levels, p % levels], dst.at[p, pl.ds(PAD, rows), :], b.loads.at[p]
         )
 
-    for p in range(planes):
-        for i in range(3):
-            load(i, p).start()
-
     barrier = pltpu.get_barrier_semaphore()
-    near = ((s >= 1, s - 1), (s >= 2, s - 2), (s < n - 1, s + 1), (s < n - 2, s + 2))
+    near = ((s >= 0, partner), (s >= 2, s - 2), (s < n - 2, s + 2))
     for there, who in near:
         @pl.when(there)
         def _():
@@ -185,52 +197,74 @@
     for bit in bits:
         pl.semaphore_signal(barrier, inc=1, device_id={"lev": across(bit)}, device_id_type=MESH_ID)
 
+    small_loads = [
+        pltpu.make_async_copy(src, dst, b.small_loads.at[i])
+        for i, (src, dst) in enumerate((
+            (decay_at, chain_decay), (gain_at, level_gain), (depth_at, mean_depth),
+            (cell_at, obs_cell), (obs_dual_at, obs_dual), (obs_var_at, obs_var),
+        ))
+    ]
+    small_loads[0].start()
+    for p in range(planes):
+        for i in range(3):
+            load(i, p).start()
+    for copy in small_loads[1:]:
+        copy.start()
+
     def edges(ref, planes):
         zero = jnp.zeros((PAD, cols), jnp.float32)
         for p in range(planes):
             ref[p, pl.ds(0, PAD), :] = zero
             ref[p, pl.ds(PAD + rows, PAD), :] = zero
 
+    def own_at(c):
+        p, r = where_in(c)
+
+        @pl.when(c % per == 0)
+        def _():
+            pltpu.make_async_copy(
+                increment.at[0, :, 0], b.inc.at[pl.ds(0, fields), pl.ds(PAD, rows), :], b.loads.at[p]
+            ).wait()
+
+        inner = pl.ds(pl.multiple_of((c % per) * part + PAD, 8), part)
+        b.own[p, r, :] = b.work[p, inner, :] * b.mult[p, inner, :] + b.inc[p, inner, :]
+
+    gives_own = jnp.logical_or(even, s < n - 1)
+
+    def give_own(c):
+        @pl.when(gives_own)
+        def _():
+            own_copy(c).start()
+
+    with jax.named_scope("greet"):
+        small_loads[0].wait()
+        for f in range(fields):
+            for l in range(levels):
+                b.decay[f * levels + l] = jnp.full((1, 128), chain_decay[0, l, f], jnp.float32)
+        own_at(0)
+        pl.semaphore_wait(barrier, len(bits) + sum(there.astype(jnp.int32) for there, _ in near))
+
+        @pl.when(odd == 1)
+        def _():
+            decay_copy.start()
+
+        @pl.when(jnp.logical_and(even, s >= 2))
+        def _():
+            decay_leg.start()
+
+    def own_next(c):
+        own_at(c)
+        give_own(c - 1)
+
+    with jax.named_scope("own"):
+        loop(1, chunks, own_next)
+        give_own(chunks - 1)
+
+    for copy in small_loads[1:]:
+        copy.wait()
     for ref in (b.inc, b.mult, b.work, b.b1):
         edges(ref, planes)
     edges(b.columns, 4)
-    for f in range(fields):
-        for l in range(levels):
-            b.decay[f * levels + l] = jnp.full((1, 128), chain_decay[0, l, f], jnp.float32)
-
-    def own_at(c):
-        p, r = where_in(c)
-
-        @pl.when(c % per == 0)
-        def _():
-            for i in range(3):
-                load(i, p).wait()
-
-        inner = pl.ds(pl.multiple_of((c % per) * part + PAD, 8), part)
-        b.own[p, r, :] = b.work[p, inner, :] * b.mult[p, inner, :] + b.inc[p, inner, :]
-
-    gives_own = jnp.logical_or(even, s < n - 1)
-
-    def give_own(c):
-        @pl.when(gives_own)
-        def _():
-            own_copy(c).start()
-
-    with jax.named_scope("greet"):
-        own_at(0)
-        pl.semaphore_wait(barrier, len(bits) + sum(there.astype(jnp.int32) for there, _ in near))
-
-    @pl.when(s >= 1)
-    def _():
-        decay_copy.start()
-
-    def own_next(c):
-        own_at(c)
-        give_own(c - 1)
-
-    with jax.named_scope("own"):
-        loop(1, chunks, own_next)
-        give_own(chunks - 1)
 
     def row_index(r0):
         return lax.broadcasted_iota(jnp.int32, (wide, cols), 0) + (r0 - PAD)
@@ -408,6 +442,11 @@
             h, u, v = state_at(b.work, l, r0)
             put(b.tangent, l, r0, forward(h, u, v, column, r0, level_gain[l], mean_depth[l]))
 
+    @pl.when(turns)
+    def _():
+        decay_leg.wait_recv()
+        decay_turn.start()
+
     with jax.named_scope("back"):
         sweep(last_back)
     below = pair - 1
@@ -435,10 +474,6 @@
         loop(0, up_cut, lambda c: tangent_leg(c, s + 2).start())
         loop(up_cut, chunks, lambda c: tangent_leg(c, s - 1).start())
 
-    @pl.when(s < n - 1)
-    def _():
-        decay_copy.wait_recv()
-
     def chain_step(c):
         p, r = where_in(c)
         d = chain_decay[0, p % levels, p // levels]
@@ -459,9 +494,9 @@
         def _():
             carried[p, r, :] = jnp.zeros((part, cols), jnp.float32)
 
-        @pl.when(jnp.logical_or(odd == 1, s < n - 2))
-        def _():
-            own_copy(c).wait_recv()
+        @pl.when(jnp.logical_and(c % per == 0, jnp.logical_or(odd == 1, s < n - 2)))
+        def _():
+            own_plane(p).wait_recv()
 
         swap = b.swap[p, r, :]
         product = b.own[p, r, :] - tangent_in[p, r, :]
@@ -475,6 +510,10 @@
             b.sent[p, r, :] = d_next * here + (jnp.where(even, swap, 0.0) - b.tangent[p, r, :])
             chain_copy(c).start()
 
+    @pl.when(s == 0)
+    def _():
+        decay_copy.wait_recv()
+
     with jax.named_scope("chain0"):
         loop(0, jnp.where(s == 0, chunks, 0), chain_step)
 
@@ -493,8 +532,12 @@
         with jax.named_scope("turn_over"):
             loop(0, across_cut, turn_across)
 
+    early = jnp.where(s == n - 1, chunks // 2, 0)
+
     @pl.when(odd == 1)
     def _():
+        loop(0, early, lambda c: adjoint_copy(c).start())
+
         @pl.when(s >= 3)
         def _():
             def turn_across(c):
@@ -504,7 +547,7 @@
             with jax.named_scope("turn_back"):
                 loop(0, here_cut, turn_across)
 
-        loop(0, chunks, lambda c: adjoint_copy(c).start())
+        loop(early, chunks, lambda c: adjoint_copy(c).start())
 
         @pl.when(s >= 3)
         def _():
@@ -514,9 +557,6 @@
 
             with jax.named_scope("turn_down"):
                 loop(down_cut, chunks, turn_down)
-
-    with jax.named_scope("chain"):
-        loop(0, jnp.where(s == 0, 0, chunks), chain_step)
 
     def block_step(i):
         c = lax.rem(i + across_cut * odd, chunks)
@@ -534,22 +574,35 @@
         def _():
             adjoint_in[p, r, :] = kept + b.added[jnp.minimum(p, levels - 1), r, :]
 
+    loop(0, jnp.where(s == n - 1, chunks, 0), block_step)
+
+    @pl.when(jnp.logical_and(s > 0, s < n - 1))
+    def _():
+        decay_copy.wait_recv()
+
+    with jax.named_scope("chain"):
+        loop(0, jnp.where(s == 0, 0, chunks), chain_step)
+
     with jax.named_scope("block"):
-        loop(0, chunks, block_step)
+        loop(0, jnp.where(s == n - 1, 0, chunks), block_step)
 
     with jax.named_scope("drain"):
         @pl.when(gives_own)
         def _():
-            loop(0, chunks, lambda c: own_copy(c).wait_send())
+            all_sent(b.own, b.swap, 0)
 
         @pl.when(s < n - 1)
         def _():
-            loop(0, chunks, lambda c: tangent_copy(c).wait_send())
+            all_sent(b.tangent, tangent_in, 1)
 
         @pl.when(s >= 1)
         def _():
-            loop(0, chunks, lambda c: adjoint_copy(c).wait_send())
+            all_sent(b.adjoint, adjoint_in, 2)
             decay_copy.wait_send()
+
+        @pl.when(turns)
+        def _():
+            decay_turn.wait_send()
 
         @pl.when(jnp.logical_and(even, s < n - 2))
         def _():
@@ -563,15 +616,14 @@
 
         @pl.when(s < n - 2)
         def _():
-            loop(0, chunks, lambda c: chain_copy(c).wait_send())
+            all_sent(b.sent, carried, 3)
 
 
 def write_out(dual_in, seen_in, block_in, chain_in, dual, seen, block, chain, sems):
-    planes = dual.shape[0]
-    copies = [pltpu.make_async_copy(seen_in, seen, sems.at[3 * planes])]
-    for i, (src, dst) in enumerate(((dual_in, dual), (block_in, block), (chain_in, chain))):
-        for p in range(planes):
-            copies.append(pltpu.make_async_copy(src.at[p], dst.at[p], sems.at[i * planes + p]))
+    copies = [
+        pltpu.make_async_copy(src, dst, sems.at[i])
+        for i, (src, dst) in enumerate(((dual_in, dual), (block_in, block), (chain_in, chain), (seen_in, seen)))
+    ]
     for copy in copies:
         copy.start()
     for copy in copies:
@@ -603,18 +655,20 @@
         *[room(planes, rows, cols)] * 7,
         room(2, tall, cols), room(rounds, tall, cols), room(tall, cols),
         room(4, rows + 2 * PAD, cols), room(levels, rows, cols),
-        room(planes, 1, 128), room(planes, 1, 128),
-        *[flags(chunks)] * 12,
-        flags(1), flags(1), flags(3 * planes), flags(rounds + 1), flags(rounds + 1),
+        *[room(planes, 1, 128)] * 3,
+        pltpu.VMEM(obs_cell.shape, jnp.int32), room(*obs_dual.shape), room(*obs_var.shape),
+        pltpu.SMEM(level_gain.shape, jnp.float32), pltpu.SMEM(mean_depth.shape, jnp.float32),
+        pltpu.SMEM((1, levels, fields), jnp.float32),
+        flags(4), *[flags(planes)] * 2, *[flags(chunks)] * 7,
+        flags(2), flags(2), flags(6), flags(rounds + 1), flags(rounds + 1),
     )
     place = pl.BlockSpec(memory_space=pl.ANY)
     small = pl.BlockSpec(memory_space=pltpu.VMEM)
-    scalar = pl.BlockSpec(memory_space=pltpu.SMEM)
     held = pltpu.VMEM((planes, rows, cols), jnp.float32)
     results = pl.pallas_call(
         functools.partial(kernel, n, size),
         out_shape=[held, pltpu.VMEM(obs_dual.shape, jnp.float32), held, held],
-        in_specs=[place] * 3 + [small] * 3 + [scalar] * 3,
+        in_specs=[place] * 9,
         out_specs=[small] * 4,
         scratch_shapes=list(scratch),
         compiler_params=pltpu.CompilerParams(
@@ -629,7 +683,7 @@
         out_shape=[jax.ShapeDtypeStruct(r.shape, jnp.float32) for r in results],
         in_specs=[small] * 4,
         out_specs=[place] * 4,
-        scratch_shapes=[flags(3 * planes + 1)],
+        scratch_shapes=[flags(4)],
         compiler_params=pltpu.CompilerParams(vmem_limit_bytes=1024 * 1024),
     )(*[pltpu.with_memory_space_constraint(r, pltpu.VMEM) for r in results])
     return (

time: 196 us -> 194 us (0.990)
  no operation moved by 1% of the time
where the time goes in v2:
time: 194 us; the launch traced here: 193 us
  Pallas kernels  192 us (99%)
    pallas_call x1, Pallas kernels, shards(): pl.pallas_call(functools.partial(kernel, n, size), out_shape=[held, pltpu...  188 us

profile of v2, /device:TPU:24, one launch (start us, length us, event | category | flops | bytes accessed | tf_op | source)
XLA Modules:
  0.0 192.6 jit_solution(5875126212504139717)
XLA Ops:
  0.6 188.2 %shard_map.120 = (f32[6,256,512]{2,1,0:T(8,128)S(1)}, f32[1,2,512]{2,1,0:T(2,128)S(1)}, f32[6,256,512]{2,1,0:T(8,128)S(1)}, f32[6,256,512]{2,1,0:T(8,128)S(1)}) custom-call(f32[1,3,2,256,512]{4,3,2,1,0:T(8,128)} %increment.1, f32[1,3,2,256,512]{4,3,2,1,0:T(8,128)} %multiplier.1, f32[1,3,2,256,512]{4,3,2,1,0:T(8,128)} %error_var.1, s32[1,2,512]{2,1,0:T(2,128)} %cell_at.1, ...), custom_call_target="tpu_custom_call" | custom-call | tf_op jit(solution)/shard_map/pallas_call | solution.py:668
  188.8 3.8 %shard_map.121 = (f32[6,256,512]{2,1,0:T(8,128)}, f32[1,2,512]{2,1,0:T(2,128)}, f32[6,256,512]{2,1,0:T(8,128)}, f32[6,256,512]{2,1,0:T(8,128)}) custom-call(f32[6,256,512]{2,1,0:T(8,128)S(1)} %get-tuple-element.12.dual_in, f32[1,2,512]{2,1,0:T(2,128)S(1)} %get-tuple-element.13.seen_in, f32[6,256,512]{2,1,0:T(8,128)S(1)} %get-tuple-element.14.block_in, ...), custom_call_target="tpu_custom_call" | custom-call | tf_op jit(solution)/shard_map/pallas_call | solution.py:681

commit v3 on v2

--- a/solution.py
+++ b/solution.py
@@ -48,9 +48,7 @@
     loads: Any
     tan_recv: Any
     adj_recv: Any
-    rt_send: Any
     rt_recv: Any
-    ra_send: Any
     ra_recv: Any
     ch_recv: Any
     decay_send: Any
@@ -114,7 +112,7 @@
         return chunks * (pairs - 1 - k) // pairs
 
     def tangent_cut(k):
-        return jnp.minimum(chunks, chunks * (k + 1) // max(pairs - 1, 1))
+        return chunks * (k + 1) // max(pairs - 1, 1)
 
     def loop(low, high, fn):
         lax.fori_loop(low, high, lambda c, z: (fn(c), z)[1], 0)
@@ -156,16 +154,16 @@
         return move(b.sent, carried, b.sends.at[3], b.ch_recv, c, s + 2)
 
     def tangent_leg(c, to):
-        return move(b.tangent, b.relay_t, b.sends.at[1], b.rt_recv, c, to)
+        return remote(piece(b.tangent, c), b.relay_t.at[c], b.sends.at[1], b.rt_recv.at[c], {"tm": to})
 
     def tangent_turn(c, to):
-        return move(b.relay_t, tangent_in, b.rt_send.at[c], b.tan_recv, c, to)
+        return remote(b.relay_t.at[c], piece(tangent_in, c), b.sends.at[4], b.tan_recv.at[c], {"tm": to})
 
     def adjoint_leg(c, to):
-        return move(b.adjoint, b.relay_a, b.sends.at[2], b.ra_recv, c, to)
+        return remote(piece(b.adjoint, c), b.relay_a.at[c], b.sends.at[2], b.ra_recv.at[c], {"tm": to})
 
     def adjoint_turn(c, to):
-        return move(b.relay_a, adjoint_in, b.ra_send.at[c], b.adj_recv, c, to)
+        return remote(b.relay_a.at[c], piece(adjoint_in, c), b.sends.at[5], b.adj_recv.at[c], {"tm": to})
 
     decay_copy = remote(b.decay, b.decay_in, b.decay_send.at[0], b.decay_recv.at[0], {"tm": s - 1})
     decay_leg = remote(b.decay, b.decay_relay, b.decay_send.at[0], b.decay_recv.at[1], {"tm": s - 2})
@@ -257,7 +255,9 @@
         give_own(c - 1)
 
     with jax.named_scope("own"):
-        loop(1, chunks, own_next)
+        give_own(0)
+        own_at(1)
+        loop(2, chunks, own_next)
         give_own(chunks - 1)
 
     for copy in small_loads[1:]:
@@ -501,13 +501,17 @@
         swap = b.swap[p, r, :]
         product = b.own[p, r, :] - tangent_in[p, r, :]
         here = d * (carried[p, r, :] + jnp.where(odd == 1, swap, 0.0)) + product
+
+        @pl.when(s < n - 2)
+        def _():
+            d_next = b.decay_in[p][:, :1]
+            b.sent[p, r, :] = d_next * here + (jnp.where(even, swap, 0.0) - b.tangent[p, r, :])
+
         tangent_in[p, r, :] = product
         carried[p, r, :] = here
 
         @pl.when(s < n - 2)
         def _():
-            d_next = b.decay_in[p][:, :1]
-            b.sent[p, r, :] = d_next * here + (jnp.where(even, swap, 0.0) - b.tangent[p, r, :])
             chain_copy(c).start()
 
     @pl.when(s == 0)
@@ -604,15 +608,20 @@
         def _():
             decay_turn.wait_send()
 
-        @pl.when(jnp.logical_and(even, s < n - 2))
-        def _():
-            loop(up_cut, chunks, lambda c: tangent_turn(c, s + 2).wait_send())
-            loop(0, across_cut, lambda c: adjoint_turn(c, s + 1).wait_send())
-
-        @pl.when(jnp.logical_and(odd == 1, s >= 3))
-        def _():
-            loop(0, here_cut, lambda c: tangent_turn(c, s - 1).wait_send())
-            loop(down_cut, chunks, lambda c: adjoint_turn(c, s - 2).wait_send())
+        def turned(ref, i, count):
+            if count:
+                all_sent(ref.at[pl.ds(0, count)], ref.at[pl.ds(0, count)], i)
+
+        for k in range(pairs - 1):
+            @pl.when(s == 2 * k)
+            def _():
+                turned(b.relay_t, 4, chunks - tangent_cut(k))
+                turned(b.relay_a, 5, adjoint_cut(k))
+
+            @pl.when(s == 2 * k + 3)
+            def _():
+                turned(b.relay_t, 4, tangent_cut(k))
+                turned(b.relay_a, 5, chunks - adjoint_cut(k))
 
         @pl.when(s < n - 2)
         def _():
@@ -652,14 +661,14 @@
 
     scratch = Scratch(
         *[room(planes, rows + 2 * PAD, cols)] * 4,
-        *[room(planes, rows, cols)] * 7,
+        *[room(planes, rows, cols)] * 5, *[room(chunks, rows // pieces(rows), cols)] * 2,
         room(2, tall, cols), room(rounds, tall, cols), room(tall, cols),
         room(4, rows + 2 * PAD, cols), room(levels, rows, cols),
         *[room(planes, 1, 128)] * 3,
         pltpu.VMEM(obs_cell.shape, jnp.int32), room(*obs_dual.shape), room(*obs_var.shape),
         pltpu.SMEM(level_gain.shape, jnp.float32), pltpu.SMEM(mean_depth.shape, jnp.float32),
         pltpu.SMEM((1, levels, fields), jnp.float32),
-        flags(4), *[flags(planes)] * 2, *[flags(chunks)] * 7,
+        flags(6), *[flags(planes)] * 2, *[flags(chunks)] * 5,
         flags(2), flags(2), flags(6), flags(rounds + 1), flags(rounds + 1),
     )
     place = pl.BlockSpec(memory_space=pl.ANY)

time: 194 us -> 194 us (level)
  no operation moved by 1% of the time
where the time goes in v3:
time: 194 us; the launch traced here: 192 us
  Pallas kernels  192 us (99%)
    pallas_call x1, Pallas kernels, shards(): pl.pallas_call(functools.partial(kernel, n, size), out_shape=[held, pltpu...  188 us

profile of v3, /device:TPU:24, one launch (start us, length us, event | category | flops | bytes accessed | tf_op | source)
XLA Modules:
  0.0 192.4 jit_solution(3040238034324709221)
XLA Ops:
  0.6 188.0 %shard_map.120 = (f32[6,256,512]{2,1,0:T(8,128)S(1)}, f32[1,2,512]{2,1,0:T(2,128)S(1)}, f32[6,256,512]{2,1,0:T(8,128)S(1)}, f32[6,256,512]{2,1,0:T(8,128)S(1)}) custom-call(f32[1,3,2,256,512]{4,3,2,1,0:T(8,128)} %increment.1, f32[1,3,2,256,512]{4,3,2,1,0:T(8,128)} %multiplier.1, f32[1,3,2,256,512]{4,3,2,1,0:T(8,128)} %error_var.1, s32[1,2,512]{2,1,0:T(2,128)} %cell_at.1, ...), custom_call_target="tpu_custom_call" | custom-call | tf_op jit(solution)/shard_map/pallas_call | solution.py:677
  188.6 3.8 %shard_map.121 = (f32[6,256,512]{2,1,0:T(8,128)}, f32[1,2,512]{2,1,0:T(2,128)}, f32[6,256,512]{2,1,0:T(8,128)}, f32[6,256,512]{2,1,0:T(8,128)}) custom-call(f32[6,256,512]{2,1,0:T(8,128)S(1)} %get-tuple-element.12.dual_in, f32[1,2,512]{2,1,0:T(2,128)S(1)} %get-tuple-element.13.seen_in, f32[6,256,512]{2,1,0:T(8,128)S(1)} %get-tuple-element.14.block_in, ...), custom_call_target="tpu_custom_call" | custom-call | tf_op jit(solution)/shard_map/pallas_call | solution.py:690

commit v4 on v3

--- a/solution.py
+++ b/solution.py
@@ -1,4 +1,3 @@
-import functools
 from typing import Any, NamedTuple
 
 import jax
@@ -12,7 +11,7 @@
 ROTATION_PARAM = 0.5
 COUPLING = 0.25
 HALF = TIME_STEP * ROTATION_PARAM
-SPLIT = 2
+SPLIT = 4
 PAD = 8
 MESH_ID = pl.DeviceIdType.MESH
 
@@ -659,7 +658,7 @@
     def flags(count):
         return pltpu.SemaphoreType.DMA((count,))
 
-    scratch = Scratch(
+    scratch = [
         *[room(planes, rows + 2 * PAD, cols)] * 4,
         *[room(planes, rows, cols)] * 5, *[room(chunks, rows // pieces(rows), cols)] * 2,
         room(2, tall, cols), room(rounds, tall, cols), room(tall, cols),
@@ -668,18 +667,24 @@
         pltpu.VMEM(obs_cell.shape, jnp.int32), room(*obs_dual.shape), room(*obs_var.shape),
         pltpu.SMEM(level_gain.shape, jnp.float32), pltpu.SMEM(mean_depth.shape, jnp.float32),
         pltpu.SMEM((1, levels, fields), jnp.float32),
+    ]
+    sems = [
         flags(6), *[flags(planes)] * 2, *[flags(chunks)] * 5,
         flags(2), flags(2), flags(6), flags(rounds + 1), flags(rounds + 1),
-    )
+    ]
+
+    def scoped(*refs):
+        pl.run_scoped(lambda *scope: kernel(n, size, *refs, *scope), *sems)
+
     place = pl.BlockSpec(memory_space=pl.ANY)
     small = pl.BlockSpec(memory_space=pltpu.VMEM)
     held = pltpu.VMEM((planes, rows, cols), jnp.float32)
     results = pl.pallas_call(
-        functools.partial(kernel, n, size),
+        scoped,
         out_shape=[held, pltpu.VMEM(obs_dual.shape, jnp.float32), held, held],
         in_specs=[place] * 9,
         out_specs=[small] * 4,
-        scratch_shapes=list(scratch),
+        scratch_shapes=scratch,
         compiler_params=pltpu.CompilerParams(
             collective_id=0, has_side_effects=True, vmem_limit_bytes=50 * 1024 * 1024
         ),

time: 194 us -> 193 us (level)
  no operation moved by 1% of the time
where the time goes in v4:
time: 193 us; the launch traced here: 192 us
  Pallas kernels  191 us (99%)
    pallas_call x1, Pallas kernels, shards(): pl.pallas_call(scoped, out_shape=[held, pltpu.VMEM(obs_dual.shape, jnp.fl...  187 us

profile of v4, /device:TPU:24, one launch (start us, length us, event | category | flops | bytes accessed | tf_op | source)
XLA Modules:
  0.0 191.5 jit_solution(15955917958578095654)
XLA Ops:
  0.6 187.1 %shard_map.120 = (f32[6,256,512]{2,1,0:T(8,128)S(1)}, f32[1,2,512]{2,1,0:T(2,128)S(1)}, f32[6,256,512]{2,1,0:T(8,128)S(1)}, f32[6,256,512]{2,1,0:T(8,128)S(1)}) custom-call(f32[1,3,2,256,512]{4,3,2,1,0:T(8,128)} %refs_0_.1, f32[1,3,2,256,512]{4,3,2,1,0:T(8,128)} %refs_1_.1, f32[1,3,2,256,512]{4,3,2,1,0:T(8,128)} %refs_2_.1, s32[1,2,512]{2,1,0:T(2,128)} %refs_3_.1, ...), custom_call_target="tpu_custom_call" | custom-call | tf_op jit(solution)/shard_map/pallas_call | solution.py:682
  187.7 3.8 %shard_map.121 = (f32[6,256,512]{2,1,0:T(8,128)}, f32[1,2,512]{2,1,0:T(2,128)}, f32[6,256,512]{2,1,0:T(8,128)}, f32[6,256,512]{2,1,0:T(8,128)}) custom-call(f32[6,256,512]{2,1,0:T(8,128)S(1)} %get-tuple-element.12.dual_in, f32[1,2,512]{2,1,0:T(2,128)S(1)} %get-tuple-element.13.seen_in, f32[6,256,512]{2,1,0:T(8,128)S(1)} %get-tuple-element.14.block_in, ...), custom_call_target="tpu_custom_call" | custom-call | tf_op jit(solution)/shard_map/pallas_call | solution.py:695

commit v5 on v4

--- a/solution.py
+++ b/solution.py
@@ -169,12 +169,19 @@
     decay_turn = remote(b.decay_relay, b.decay_in, b.decay_send.at[1], b.decay_recv.at[0], {"tm": s + 1})
     turns = jnp.logical_and(even, s < n - 2)
 
-    def load(i, p):
+    def load(i, p, low, high, sem):
         src = (increment, multiplier, error_var)[i]
         dst = (b.inc, b.mult, b.work)[i]
         return pltpu.make_async_copy(
-            src.at[0, p // levels, p % levels], dst.at[p, pl.ds(PAD, rows), :], b.loads.at[p]
+            src.at[0, p // levels, p % levels, pl.ds(low, high - low), :],
+            dst.at[p, pl.ds(PAD + low, high - low), :], b.loads.at[sem],
         )
+
+    def loaded(low, high, sem):
+        pltpu.make_async_copy(
+            increment.at[0, :, 0, pl.ds(low, high - low), :],
+            b.inc.at[pl.ds(0, fields), pl.ds(PAD + low, high - low), :], b.loads.at[sem],
+        ).wait()
 
     barrier = pltpu.get_barrier_semaphore()
     near = ((s >= 0, partner), (s >= 2, s - 2), (s < n - 2, s + 2))
@@ -201,10 +208,14 @@
             (cell_at, obs_cell), (obs_dual_at, obs_dual), (obs_var_at, obs_var),
         ))
     ]
+    for i in range(3):
+        load(i, 0, 0, part, planes).start()
     small_loads[0].start()
     for p in range(planes):
-        for i in range(3):
-            load(i, p).start()
+        low = part if p == 0 else 0
+        if low < rows:
+            for i in range(3):
+                load(i, p, low, rows, p).start()
     for copy in small_loads[1:]:
         copy.start()
 
@@ -217,11 +228,17 @@
     def own_at(c):
         p, r = where_in(c)
 
-        @pl.when(c % per == 0)
-        def _():
-            pltpu.make_async_copy(
-                increment.at[0, :, 0], b.inc.at[pl.ds(0, fields), pl.ds(PAD, rows), :], b.loads.at[p]
-            ).wait()
+        if isinstance(c, int):
+            if c == 0:
+                loaded(0, part, planes)
+            elif c == 1 and per > 1:
+                loaded(part, rows, 0)
+            else:
+                loaded(0, rows, p)
+        else:
+            @pl.when(c % per == 0)
+            def _():
+                loaded(0, rows, p)
 
         inner = pl.ds(pl.multiple_of((c % per) * part + PAD, 8), part)
         b.own[p, r, :] = b.work[p, inner, :] * b.mult[p, inner, :] + b.inc[p, inner, :]
@@ -234,12 +251,20 @@
             own_copy(c).start()
 
     with jax.named_scope("greet"):
+        own_at(0)
+        pl.semaphore_wait(barrier, len(bits) + sum(there.astype(jnp.int32) for there, _ in near))
+
+    def own_next(c):
+        own_at(c)
+        give_own(c - 1)
+
+    with jax.named_scope("own"):
+        give_own(0)
+        own_at(1)
         small_loads[0].wait()
         for f in range(fields):
             for l in range(levels):
                 b.decay[f * levels + l] = jnp.full((1, 128), chain_decay[0, l, f], jnp.float32)
-        own_at(0)
-        pl.semaphore_wait(barrier, len(bits) + sum(there.astype(jnp.int32) for there, _ in near))
 
         @pl.when(odd == 1)
         def _():
@@ -249,13 +274,6 @@
         def _():
             decay_leg.start()
 
-    def own_next(c):
-        own_at(c)
-        give_own(c - 1)
-
-    with jax.named_scope("own"):
-        give_own(0)
-        own_at(1)
         loop(2, chunks, own_next)
         give_own(chunks - 1)
 
@@ -627,15 +645,18 @@
             all_sent(b.sent, carried, 3)
 
 
-def write_out(dual_in, seen_in, block_in, chain_in, dual, seen, block, chain, sems):
-    copies = [
-        pltpu.make_async_copy(src, dst, sems.at[i])
-        for i, (src, dst) in enumerate(((dual_in, dual), (block_in, block), (chain_in, chain), (seen_in, seen)))
-    ]
-    for copy in copies:
-        copy.start()
-    for copy in copies:
-        copy.wait()
+def write_out(dual_in, seen_in, block_in, chain_in, dual, seen, block, chain):
+    def copy_all(sems):
+        copies = [
+            pltpu.make_async_copy(src, dst, sems.at[i])
+            for i, (src, dst) in enumerate(((dual_in, dual), (block_in, block), (chain_in, chain), (seen_in, seen)))
+        ]
+        for copy in copies:
+            copy.start()
+        for copy in copies:
+            copy.wait()
+
+    pl.run_scoped(copy_all, pltpu.SemaphoreType.DMA((4,)))
 
 
 def shards(
@@ -669,7 +690,7 @@
         pltpu.SMEM((1, levels, fields), jnp.float32),
     ]
     sems = [
-        flags(6), *[flags(planes)] * 2, *[flags(chunks)] * 5,
+        flags(6), flags(planes), flags(planes + 1), *[flags(chunks)] * 5,
         flags(2), flags(2), flags(6), flags(rounds + 1), flags(rounds + 1),
     ]
 
@@ -697,7 +718,6 @@
         out_shape=[jax.ShapeDtypeStruct(r.shape, jnp.float32) for r in results],
         in_specs=[small] * 4,
         out_specs=[place] * 4,
-        scratch_shapes=[flags(4)],
         compiler_params=pltpu.CompilerParams(vmem_limit_bytes=1024 * 1024),
     )(*[pltpu.with_memory_space_constraint(r, pltpu.VMEM) for r in results])
     return (

time: 193 us -> 193 us (level)
  no operation moved by 1% of the time
where the time goes in v5:
time: 193 us; the launch traced here: 191 us
  Pallas kernels  191 us (99%)
    pallas_call x1, Pallas kernels, shards(): pl.pallas_call(scoped, out_shape=[held, pltpu.VMEM(obs_dual.shape, jnp.fl...  187 us

profile of v5, /device:TPU:24, one launch (start us, length us, event | category | flops | bytes accessed | tf_op | source)
XLA Modules:
  0.0 191.3 jit_solution(4209099095154743825)
XLA Ops:
  0.6 186.9 %shard_map.120 = (f32[6,256,512]{2,1,0:T(8,128)S(1)}, f32[1,2,512]{2,1,0:T(2,128)S(1)}, f32[6,256,512]{2,1,0:T(8,128)S(1)}, f32[6,256,512]{2,1,0:T(8,128)S(1)}) custom-call(f32[1,3,2,256,512]{4,3,2,1,0:T(8,128)} %refs_0_.1, f32[1,3,2,256,512]{4,3,2,1,0:T(8,128)} %refs_1_.1, f32[1,3,2,256,512]{4,3,2,1,0:T(8,128)} %refs_2_.1, s32[1,2,512]{2,1,0:T(2,128)} %refs_3_.1, ...), custom_call_target="tpu_custom_call" | custom-call | tf_op jit(solution)/shard_map/pallas_call | solution.py:703
  187.6 3.7 %shard_map.121 = (f32[6,256,512]{2,1,0:T(8,128)}, f32[1,2,512]{2,1,0:T(2,128)}, f32[6,256,512]{2,1,0:T(8,128)}, f32[6,256,512]{2,1,0:T(8,128)}) custom-call(f32[6,256,512]{2,1,0:T(8,128)S(1)} %get-tuple-element.12.dual_in, f32[1,2,512]{2,1,0:T(2,128)S(1)} %get-tuple-element.13.seen_in, f32[6,256,512]{2,1,0:T(8,128)S(1)} %get-tuple-element.14.block_in, ...), custom_call_target="tpu_custom_call" | custom-call | tf_op jit(solution)/shard_map/pallas_call | solution.py:716

commit v6 on v5

--- a/solution.py
+++ b/solution.py
@@ -11,7 +11,7 @@
 ROTATION_PARAM = 0.5
 COUPLING = 0.25
 HALF = TIME_STEP * ROTATION_PARAM
-SPLIT = 4
+SPLIT = 8
 PAD = 8
 MESH_ID = pl.DeviceIdType.MESH
 
@@ -651,8 +651,8 @@
             pltpu.make_async_copy(src, dst, sems.at[i])
             for i, (src, dst) in enumerate(((dual_in, dual), (block_in, block), (chain_in, chain), (seen_in, seen)))
         ]
-        for copy in copies:
-            copy.start()
+        for i, copy in enumerate(copies):
+            copy.start(priority=i % 2)
         for copy in copies:
             copy.wait()
 

time: 193 us -> 193 us (level)
  no operation moved by 1% of the time
where the time goes in v6:
time: 193 us; the launch traced here: 191 us
  Pallas kernels  191 us (99%)
    pallas_call x1, Pallas kernels, shards(): pl.pallas_call(scoped, out_shape=[held, pltpu.VMEM(obs_dual.shape, jnp.fl...  187 us

profile of v6, /device:TPU:24, one launch (start us, length us, event | category | flops | bytes accessed | tf_op | source)
XLA Modules:
  0.0 191.2 jit_solution(11472996244251197632)
XLA Ops:
  0.6 186.9 %shard_map.120 = (f32[6,256,512]{2,1,0:T(8,128)S(1)}, f32[1,2,512]{2,1,0:T(2,128)S(1)}, f32[6,256,512]{2,1,0:T(8,128)S(1)}, f32[6,256,512]{2,1,0:T(8,128)S(1)}) custom-call(f32[1,3,2,256,512]{4,3,2,1,0:T(8,128)} %refs_0_.1, f32[1,3,2,256,512]{4,3,2,1,0:T(8,128)} %refs_1_.1, f32[1,3,2,256,512]{4,3,2,1,0:T(8,128)} %refs_2_.1, s32[1,2,512]{2,1,0:T(2,128)} %refs_3_.1, ...), custom_call_target="tpu_custom_call" | custom-call | tf_op jit(solution)/shard_map/pallas_call | solution.py:703
  187.6 3.6 %shard_map.121 = (f32[6,256,512]{2,1,0:T(8,128)}, f32[1,2,512]{2,1,0:T(2,128)}, f32[6,256,512]{2,1,0:T(8,128)}, f32[6,256,512]{2,1,0:T(8,128)}) custom-call(f32[6,256,512]{2,1,0:T(8,128)S(1)} %get-tuple-element.12.dual_in, f32[1,2,512]{2,1,0:T(2,128)S(1)} %get-tuple-element.13.seen_in, f32[6,256,512]{2,1,0:T(8,128)S(1)} %get-tuple-element.14.block_in, ...), custom_call_target="tpu_custom_call" | custom-call | tf_op jit(solution)/shard_map/pallas_call | solution.py:716

commit v7 on v6

--- a/solution.py
+++ b/solution.py
@@ -652,7 +652,7 @@
             for i, (src, dst) in enumerate(((dual_in, dual), (block_in, block), (chain_in, chain), (seen_in, seen)))
         ]
         for i, copy in enumerate(copies):
-            copy.start(priority=i % 2)
+            copy.start(priority=(i + 1) % 2)
         for copy in copies:
             copy.wait()
 

time: 193 us -> 193 us (level)
  no operation moved by 1% of the time
where the time goes in v7:
time: 193 us; the launch traced here: 191 us
  Pallas kernels  191 us (99%)
    pallas_call x1, Pallas kernels, shards(): pl.pallas_call(scoped, out_shape=[held, pltpu.VMEM(obs_dual.shape, jnp.fl...  187 us

profile of v7, /device:TPU:24, one launch (start us, length us, event | category | flops | bytes accessed | tf_op | source)
XLA Modules:
  0.0 191.3 jit_solution(13099274623999161319)
XLA Ops:
  0.6 186.9 %shard_map.120 = (f32[6,256,512]{2,1,0:T(8,128)S(1)}, f32[1,2,512]{2,1,0:T(2,128)S(1)}, f32[6,256,512]{2,1,0:T(8,128)S(1)}, f32[6,256,512]{2,1,0:T(8,128)S(1)}) custom-call(f32[1,3,2,256,512]{4,3,2,1,0:T(8,128)} %refs_0_.1, f32[1,3,2,256,512]{4,3,2,1,0:T(8,128)} %refs_1_.1, f32[1,3,2,256,512]{4,3,2,1,0:T(8,128)} %refs_2_.1, s32[1,2,512]{2,1,0:T(2,128)} %refs_3_.1, ...), custom_call_target="tpu_custom_call" | custom-call | tf_op jit(solution)/shard_map/pallas_call | solution.py:703
  187.6 3.7 %shard_map.121 = (f32[6,256,512]{2,1,0:T(8,128)}, f32[1,2,512]{2,1,0:T(2,128)}, f32[6,256,512]{2,1,0:T(8,128)}, f32[6,256,512]{2,1,0:T(8,128)}) custom-call(f32[6,256,512]{2,1,0:T(8,128)S(1)} %get-tuple-element.12.dual_in, f32[1,2,512]{2,1,0:T(2,128)S(1)} %get-tuple-element.13.seen_in, f32[6,256,512]{2,1,0:T(8,128)S(1)} %get-tuple-element.14.block_in, ...), custom_call_target="tpu_custom_call" | custom-call | tf_op jit(solution)/shard_map/pallas_call | solution.py:716
